TPU v7x, 256 devices: a whole 4x4x8 slice. The times are simulated.
256 devices in a mesh: gx: 16 (over z, x_lo), gy: 16 (over y, x_hi, core).
Axes of the slice: x: 4 (x_hi: 2, x_lo: 2; x = x_hi * 2 + x_lo), y: 4, z: 8, core: 2. Of those that a mesh axis runs over, the one named last changes fastest.
Arguments:
- gradient: float32 [2048, 512], P('gx', 'gy'), may hold values from -6 to 6
- stat_old: float32 [2048, 2048], P('gx', 'gy'), may hold values from -1.001 to 1.001, as said below
Outputs:
- statistic: float32 [2048, 2048], P('gx', 'gy')
- inverse_root: float32 [2048, 2048], P('gx', 'gy')
Inputs may be any that keep to these rules, and one draw needn't show every extreme that they name: stat_old is symmetric positive semidefinite with unit diagonal, the Gram matrix of 2048 unit-length rows of 512 entries.
All inputs are finite; a program needn't handle non-finite values.
Results may differ from a plain program's by a relative error of at most 0.0003.
Values sent between devices are 32-bit elements.
A program may use at most 64 MiB of HBM per device.

v0:
```python
import jax
import jax.numpy as jnp
from jax import lax
from jax.sharding import Mesh
from jax.sharding import PartitionSpec as P

GY = ("gy_0", "gy_1", "gy_2")
GX = ("gx_0", "gx_1")
GX_GY = ("gx_0", "gx_1", "gy_0", "gy_1", "gy_2")


def gather_axes(array, axes, dim):
    filled = array
    for number in range(len(axes) - 1, -1, -1):
        filled = lax.all_gather(filled, axes[number], axis=dim, tiled=True)
    return filled


def folded(array, axes, dim, take_in, carry):
    everything = jax.tree.map(lambda part: gather_axes(part, axes, dim), array)
    return take_in(carry, everything, jnp.int32(0))


def spread(array, axes, root):
    array = jnp.where(lax.axis_index(axes) == root, array, jnp.zeros_like(array))
    for axis in axes:
        array = lax.psum(array, axis)
    return array


def over_axes(array, axes):
    for axis in axes:
        array = lax.psum(array, axis)
    return array


def matmul(leading, trailing):
    return jnp.dot(
        leading, trailing, preferred_element_type=jnp.float32, precision=lax.Precision.HIGHEST
    )


def panels(factor_one, factor_two):
    whole_row = lax.all_gather(factor_one, GY, axis=1, tiled=True)

    def accumulate(running, shard_rows, first_row):
        matching = lax.dynamic_slice_in_dim(whole_row, first_row, shard_rows.shape[0], 1)
        return running + matmul(matching, shard_rows)

    empty = jnp.zeros((factor_one.shape[0], factor_two.shape[1]), jnp.float32)
    return folded(factor_two, GX, 0, accumulate, empty)


def product(factor_one, factor_two):
    return panels(factor_one, factor_two)


def local(gradient, stat_old):
    count_rows = lax.axis_size(GX)
    count_cols = lax.axis_size(GY)
    factor = count_rows // count_cols
    piece_width = stat_old.shape[0]
    row_index = lax.axis_index(GX)
    col_index = lax.axis_index(GY)
    panel_rows = lax.all_gather(gradient, GY, axis=1, tiled=True)
    outer_parts = []
    for member in range(factor):
        column_rows = spread(panel_rows, GX, col_index * factor + member)
        outer_parts.append(matmul(panel_rows, column_rows.T))
    outer = jnp.concatenate(outer_parts, axis=1) / panel_rows.shape[1]
    statistic = 0.9 * stat_old + outer
    squares = over_axes(jnp.sum(statistic * statistic), GX_GY)
    divisor = 2.0 * jnp.sqrt(squares / (piece_width * count_rows))
    global_rows = row_index * piece_width + lax.broadcasted_iota(jnp.int32, stat_old.shape, 0)
    global_cols = col_index * (factor * piece_width) + lax.broadcasted_iota(
        jnp.int32, stat_old.shape, 1
    )
    identity = (global_rows == global_cols).astype(jnp.float32)
    normed = statistic / divisor
    first_step = 1.5 * identity - 0.5 * normed
    root_half = product(normed, first_step)
    product_mid = product(first_step, root_half)
    second_step = 1.5 * identity - 0.5 * product_mid
    inverse_root = product(second_step, first_step)
    return (statistic, inverse_root)


def solution(mesh):
    torus = Mesh(mesh.devices.reshape(8, 2, 4, 2, 2), ("gx_0", "gx_1", "gy_0", "gy_1", "gy_2"))
    placed = (P(GX, GY), P(GX, GY))
    return jax.shard_map(
        local, mesh=torus, in_specs=placed, out_specs=(P(GX, GY), P(GX, GY)), check_vma=False
    )
```

profile of v0, /device:TPU:1, one launch (start us, length us, event | category | flops | bytes accessed | tf_op | source)
XLA Modules:
  0.0 435.5 jit_solution(8363940582427046131)
XLA Ops:
  7.2 0.0 copy-start.3
  7.2 0.0 all-reduce.3.cloned.1.call-start
  7.2 0.7 copy-done.3
  7.9 26.8 %all_gather.26 = f32[128,512]{0,1:T(8,128)S(1)} all-gather(f32[128,32]{0,1:T(8,128)S(1)} %copy-done.3), channel_id=1, replica_groups=mesh['gx_0'=8,'gx_1'=2,'gy_0'=4,'gy_1'=2,'gy_2'=2] {'gy_0','gy_1','gy_2'}, dimensions={1}, use_global_device_ids=true | all-gather | bytes 278528 | tf_op jit(solution)/shard_map/all_gather | solution.py:65
  34.6 0.7 broadcast_select_fusion
  35.4 0.0 all-reduce.3.cloned.1.call-update
  35.4 0.0 all-reduce.5.cloned.1.call-start
  35.4 65.4 %all-reduce.3.cloned.1.call-done = f32[128,512]{0,1:T(8,128)} async-done(((f32[128,512]{0,1:T(8,128)}), f32[128,512]{0,1:T(8,128)}) %all-reduce.3.cloned.1.call-update) | async-done | bytes 262160 | tf_op jit(solution)/shard_map/psum | solution.py:27
  100.8 0.0 copy-start.2
  100.8 0.0 all-reduce.5.cloned.1.call-update
  100.8 0.0 all-gather.10.cloned.1.call-start
  100.9 0.8 copy-done.2
  101.6 0.1 copy.4
  101.7 39.7 %all-reduce.5.cloned.1.call-done = f32[128,512]{0,1:T(8,128)} async-done(((f32[128,512]{0,1:T(8,128)}), f32[128,512]{0,1:T(8,128)}) %all-reduce.5.cloned.1.call-update) | async-done | bytes 262160 | tf_op jit(solution)/shard_map/psum | solution.py:27
  141.4 2.1 multiply_reduce_fusion
  143.6 14.6 %psum.51 = f32[]{:T(128)} all-reduce(f32[]{:T(128)} %get-tuple-element.6), channel_id=1, replica_groups=mesh['gx_0'=8,'gx_1'=2,'gy_0'=4,'gy_1'=2,'gy_2'=2] {'gx_0'}, use_global_device_ids=true, to_apply=%region_3.4 | all-reduce | flops 1 | bytes 8 | tf_op jit(solution)/shard_map/psum | solution.py:33
  158.1 4.4 %psum.52 = f32[]{:T(128)} all-reduce(f32[]{:T(128)} %psum.51), channel_id=1, replica_groups=mesh['gx_0'=8,'gx_1'=2,'gy_0'=4,'gy_1'=2,'gy_2'=2] {'gx_1'}, use_global_device_ids=true, to_apply=%region_4.5 | all-reduce | flops 1 | bytes 8 | tf_op jit(solution)/shard_map/psum | solution.py:33
  162.5 9.1 %psum.53 = f32[]{:T(128)} all-reduce(f32[]{:T(128)} %psum.52), channel_id=1, replica_groups=mesh['gx_0'=8,'gx_1'=2,'gy_0'=4,'gy_1'=2,'gy_2'=2] {'gy_0'}, use_global_device_ids=true, to_apply=%region_5.6 | all-reduce | flops 1 | bytes 8 | tf_op jit(solution)/shard_map/psum | solution.py:33
  171.6 5.9 %psum.54 = f32[]{:T(128)} all-reduce(f32[]{:T(128)} %psum.53), channel_id=1, replica_groups=mesh['gx_0'=8,'gx_1'=2,'gy_0'=4,'gy_1'=2,'gy_2'=2] {'gy_1'}, use_global_device_ids=true, to_apply=%region_6.7 | all-reduce | flops 1 | bytes 8 | tf_op jit(solution)/shard_map/psum | solution.py:33
  177.5 11.8 %psum.55 = f32[]{:T(128)} all-reduce(f32[]{:T(128)} %psum.54), channel_id=1, replica_groups=mesh['gx_0'=8,'gx_1'=2,'gy_0'=4,'gy_1'=2,'gy_2'=2] {'gy_2'}, use_global_device_ids=true, to_apply=%region_7.8 | all-reduce | flops 1 | bytes 8 | tf_op jit(solution)/shard_map/psum | solution.py:33
  190.0 0.6 select_subtract_fusion
  190.6 0.0 copy-start.1
  190.6 3.9 all_gather.29
  194.5 0.0 copy-done.1
  194.5 0.0 all-gather.10.cloned.1.call-update
  194.5 0.0 all-gather.8.cloned.1.call-start
  194.6 0.5 all-gather.8.cloned.1.call-update
  195.1 0.0 all-gather.6.cloned.1.call-start
  195.1 0.5 all-gather.6.cloned.1.call-update
  195.7 0.0 all-gather.12.cloned.1.call-start
  195.7 29.4 %all-gather.10.cloned.1.call-done = f32[2048,128]{0,1:T(8,128)} async-done(((f32[256,128]{0,1:T(8,128)}), f32[2048,128]{0,1:T(8,128)}) %all-gather.10.cloned.1.call-update) | async-done | bytes 1048592 | tf_op jit(solution)/shard_map/all_gather | solution.py:15
  225.1 56.8 %all-gather.8.cloned.1.call-done = f32[128,2048]{0,1:T(8,128)} async-done(((f32[128,128]{0,1:T(8,128)}), f32[128,2048]{0,1:T(8,128)}) %all-gather.8.cloned.1.call-update) | async-done | bytes 1048592 | tf_op jit(solution)/shard_map/all_gather | solution.py:44
  281.9 3.4 fusion.3
  285.2 3.9 all_gather.31
  289.1 0.0 all-gather.12.cloned.1.call-update
  289.1 0.0 copy-start
  289.1 0.0 all-gather.14.cloned.1.call-start
  289.2 44.5 %all-gather.6.cloned.1.call-done = f32[128,2048]{0,1:T(8,128)} async-done(((f32[128,128]{0,1:T(8,128)}), f32[128,2048]{0,1:T(8,128)}) %all-gather.6.cloned.1.call-update) | async-done | bytes 1048592 | tf_op jit(solution)/shard_map/all_gather | solution.py:44
  333.7 33.6 %all-gather.12.cloned.1.call-done = f32[2048,128]{1,0:T(8,128)} async-done(((f32[256,128]{1,0:T(8,128)}), f32[2048,128]{1,0:T(8,128)}) %all-gather.12.cloned.1.call-update) | async-done | bytes 1048592 | tf_op jit(solution)/shard_map/all_gather | solution.py:15
  367.3 4.0 fusion
  371.3 0.0 all-gather.14.cloned.1.call-update
  371.3 0.7 copy.5
  372.0 53.0 %all-gather.14.cloned.1.call-done = f32[128,2048]{0,1:T(8,128)} async-done(((f32[128,128]{0,1:T(8,128)}), f32[128,2048]{0,1:T(8,128)}) %all-gather.14.cloned.1.call-update) | async-done | bytes 1048592 | tf_op jit(solution)/shard_map/all_gather | solution.py:44
  425.0 0.0 copy-done
  425.0 3.7 fusion.4
  (1 shorter events, 0.0 us)
Async XLA Ops:
  7.2 0.7 copy-start.3
  7.2 93.6 %all-reduce.3.cloned.1.call-start = ((), (), s32[]{:S(2)}) async-start(), calls=%async_computation | async-start | bytes 524288 | tf_op jit(solution)/shard_map/psum | solution.py:27
  35.4 106.1 %all-reduce.5.cloned.1.call-start = ((), (), s32[]{:S(2)}) async-start(), calls=%async_computation.1 | async-start | bytes 524288 | tf_op jit(solution)/shard_map/psum | solution.py:27
  100.8 0.8 copy-start.2
  100.8 124.2 %all-gather.10.cloned.1.call-start = ((), (), s32[]{:S(2)}) async-start(), calls=%async_computation.4 | async-start | bytes 1179648 | tf_op jit(solution)/shard_map/all_gather | solution.py:15
  190.6 3.9 copy-start.1
  194.5 87.3 %all-gather.8.cloned.1.call-start = ((), (), s32[]{:S(2)}) async-start(), calls=%async_computation.3 | async-start | bytes 1114112 | tf_op jit(solution)/shard_map/all_gather | solution.py:44
  195.1 138.6 %all-gather.6.cloned.1.call-start = ((), (), s32[]{:S(2)}) async-start(), calls=%async_computation.2 | async-start | bytes 1114112 | tf_op jit(solution)/shard_map/all_gather | solution.py:44
  195.7 171.6 %all-gather.12.cloned.1.call-start = ((), (), s32[]{:S(2)}) async-start(), calls=%async_computation.5 | async-start | bytes 1179648 | tf_op jit(solution)/shard_map/all_gather | solution.py:15
  289.1 135.9 %copy-start = (f32[2048,128]{0,1:T(8,128)S(1)}, f32[2048,128]{0,1:T(8,128)}, u32[]{:S(2)}) copy-start(f32[2048,128]{0,1:T(8,128)} %all-gather.10.cloned.1.call-done) | copy-start | bytes 3145732
  289.1 135.9 %all-gather.14.cloned.1.call-start = ((), (), s32[]{:S(2)}) async-start(), calls=%async_computation.6 | async-start | bytes 1114112 | tf_op jit(solution)/shard_map/all_gather | solution.py:44
Sparse Core Ops, SparseCore 0:
  35.5 65.2 all-reduce.2
  103.4 38.0 all-reduce.4
  194.6 30.4 all-gather.9
  228.3 53.5 all-gather.7
  285.0 48.6 all-gather.5
  335.4 31.8 all-gather.11
  371.4 53.5 all-gather.13
where the time goes:
time: 436 us
  waiting for transfers between devices  323 us (74%)
  blocking collectives  80.2 us (18%)
  between operations  14.9 us (3%)
  matrix products  13.2 us (3%)
    all_gather x3, waiting for transfers between devices, panels(): whole_row = lax.all_gather(factor_one, GY, axis=1, tiled=True)  154 us
    psum x2, waiting for transfers between devices, spread(): array = lax.psum(array, axis)  105 us
    all_gather x2, waiting for transfers between devices, gather_axes(): filled = lax.all_gather(filled, axes[number], axis=dim, tiled=True)  62.9 us
    psum x5, blocking collectives, over_axes(): array = lax.psum(array, axis)  45.7 us
    all_gather x1, blocking collectives, local(): panel_rows = lax.all_gather(gradient, GY, axis=1, tiled=True)  26.8 us
    dot_general x4, matrix products, matmul(): jnp.dot(leading, trailing, preferred_element_type=jnp.float32, precision=...  13.2 us
  transfers between devices with their start and end apart: 7, of which 7 were waited for; matrix products, arithmetic and copies ran while one was open for 1% of the time, Pallas kernels for 0%

commit v1 on v0

--- a/solution.py
+++ b/solution.py
@@ -62,7 +62,8 @@
     piece_width = stat_old.shape[0]
     row_index = lax.axis_index(GX)
     col_index = lax.axis_index(GY)
-    panel_rows = lax.all_gather(gradient, GY, axis=1, tiled=True)
+    blocks = lax.all_gather(gradient, GY)
+    panel_rows = jnp.concatenate(blocks, axis=1)
     outer_parts = []
     for member in range(factor):
         column_rows = spread(panel_rows, GX, col_index * factor + member)

time: 436 us -> 436 us (level)
  no operation moved by 1% of the time
where the time goes in v1:
time: 436 us
  waiting for transfers between devices  323 us (74%)
  blocking collectives  80.2 us (18%)
  between operations  14.9 us (3%)
  matrix products  13.2 us (3%)
    all_gather x3, waiting for transfers between devices, panels(): whole_row = lax.all_gather(factor_one, GY, axis=1, tiled=True)  154 us
    psum x2, waiting for transfers between devices, spread(): array = lax.psum(array, axis)  105 us
    all_gather x2, waiting for transfers between devices, gather_axes(): filled = lax.all_gather(filled, axes[number], axis=dim, tiled=True)  62.9 us
    psum x5, blocking collectives, over_axes(): array = lax.psum(array, axis)  45.7 us
    all_gather x1, blocking collectives, local(): blocks = lax.all_gather(gradient, GY)  26.8 us
    dot_general x4, matrix products, matmul(): jnp.dot(leading, trailing, preferred_element_type=jnp.float32, precision=...  13.2 us
  transfers between devices with their start and end apart: 7, of which 7 were waited for; matrix products, arithmetic and copies ran while one was open for 1% of the time, Pallas kernels for 0%

profile of v1, /device:TPU:1, one launch (start us, length us, event | category | flops | bytes accessed | tf_op | source)
XLA Modules:
  0.0 435.7 jit_solution(8314178923199854298)
XLA Ops:
  7.2 0.0 copy-start.3
  7.2 0.0 all-reduce.3.cloned.1.call-start
  7.2 0.7 copy-done.3
  7.9 26.8 %all-gather = f32[2048,32]{0,1:T(8,128)S(1)} all-gather(f32[128,32]{0,1:T(8,128)S(1)} %copy-done.3), channel_id=2, replica_groups=mesh['gx_0'=8,'gx_1'=2,'gy_0'=4,'gy_1'=2,'gy_2'=2] {'gy_0','gy_1','gy_2'}, dimensions={0}, use_global_device_ids=true | all-gather | bytes 278528 | tf_op jit(solution)/shard_map/all_gather | solution.py:65
  34.7 0.1 copy.9
  34.8 0.7 broadcast_select_fusion
  35.5 0.0 all-reduce.3.cloned.1.call-update
  35.6 0.0 all-reduce.5.cloned.1.call-start
  35.6 65.4 %all-reduce.3.cloned.1.call-done = f32[128,512]{0,1:T(8,128)} async-done(((f32[128,512]{0,1:T(8,128)}), f32[128,512]{0,1:T(8,128)}) %all-reduce.3.cloned.1.call-update) | async-done | bytes 262160 | tf_op jit(solution)/shard_map/psum | solution.py:27
  101.0 0.0 copy-start.2
  101.0 0.0 all-reduce.5.cloned.1.call-update
  101.0 0.0 all-gather.11.cloned.1.call-start
  101.0 0.8 copy-done.2
  101.8 0.1 copy.8
  101.9 39.7 %all-reduce.5.cloned.1.call-done = f32[128,512]{0,1:T(8,128)} async-done(((f32[128,512]{0,1:T(8,128)}), f32[128,512]{0,1:T(8,128)}) %all-reduce.5.cloned.1.call-update) | async-done | bytes 262160 | tf_op jit(solution)/shard_map/psum | solution.py:27
  141.6 2.1 multiply_reduce_fusion
  143.8 14.6 %psum.51 = f32[]{:T(128)} all-reduce(f32[]{:T(128)} %get-tuple-element.10), channel_id=1, replica_groups=mesh['gx_0'=8,'gx_1'=2,'gy_0'=4,'gy_1'=2,'gy_2'=2] {'gx_0'}, use_global_device_ids=true, to_apply=%region_3.4 | all-reduce | flops 1 | bytes 8 | tf_op jit(solution)/shard_map/psum | solution.py:33
  158.3 4.4 %psum.52 = f32[]{:T(128)} all-reduce(f32[]{:T(128)} %psum.51), channel_id=1, replica_groups=mesh['gx_0'=8,'gx_1'=2,'gy_0'=4,'gy_1'=2,'gy_2'=2] {'gx_1'}, use_global_device_ids=true, to_apply=%region_4.5 | all-reduce | flops 1 | bytes 8 | tf_op jit(solution)/shard_map/psum | solution.py:33
  162.7 9.1 %psum.53 = f32[]{:T(128)} all-reduce(f32[]{:T(128)} %psum.52), channel_id=1, replica_groups=mesh['gx_0'=8,'gx_1'=2,'gy_0'=4,'gy_1'=2,'gy_2'=2] {'gy_0'}, use_global_device_ids=true, to_apply=%region_5.6 | all-reduce | flops 1 | bytes 8 | tf_op jit(solution)/shard_map/psum | solution.py:33
  171.8 5.9 %psum.54 = f32[]{:T(128)} all-reduce(f32[]{:T(128)} %psum.53), channel_id=1, replica_groups=mesh['gx_0'=8,'gx_1'=2,'gy_0'=4,'gy_1'=2,'gy_2'=2] {'gy_1'}, use_global_device_ids=true, to_apply=%region_6.7 | all-reduce | flops 1 | bytes 8 | tf_op jit(solution)/shard_map/psum | solution.py:33
  177.7 11.8 %psum.55 = f32[]{:T(128)} all-reduce(f32[]{:T(128)} %psum.54), channel_id=1, replica_groups=mesh['gx_0'=8,'gx_1'=2,'gy_0'=4,'gy_1'=2,'gy_2'=2] {'gy_2'}, use_global_device_ids=true, to_apply=%region_7.8 | all-reduce | flops 1 | bytes 8 | tf_op jit(solution)/shard_map/psum | solution.py:33
  190.1 0.6 select_subtract_fusion
  190.8 0.0 copy-start.1
  190.8 3.9 all_gather.33
  194.6 0.0 copy-done.1
  194.6 0.0 all-gather.11.cloned.1.call-update
  194.7 0.0 all-gather.9.cloned.1.call-start
  194.7 0.5 all-gather.9.cloned.1.call-update
  195.2 0.0 all-gather.7.cloned.1.call-start
  195.3 0.5 all-gather.7.cloned.1.call-update
  195.8 0.0 all-gather.13.cloned.1.call-start
  195.9 29.4 %all-gather.11.cloned.1.call-done = f32[2048,128]{0,1:T(8,128)} async-done(((f32[256,128]{0,1:T(8,128)}), f32[2048,128]{0,1:T(8,128)}) %all-gather.11.cloned.1.call-update) | async-done | bytes 1048592 | tf_op jit(solution)/shard_map/all_gather | solution.py:15
  225.2 56.8 %all-gather.9.cloned.1.call-done = f32[128,2048]{0,1:T(8,128)} async-done(((f32[128,128]{0,1:T(8,128)}), f32[128,2048]{0,1:T(8,128)}) %all-gather.9.cloned.1.call-update) | async-done | bytes 1048592 | tf_op jit(solution)/shard_map/all_gather | solution.py:44
  282.0 3.4 fusion.3
  285.4 3.9 all_gather.35
  289.3 0.0 all-gather.13.cloned.1.call-update
  289.3 0.0 copy-start
  289.3 0.0 all-gather.15.cloned.1.call-start
  289.4 44.5 %all-gather.7.cloned.1.call-done = f32[128,2048]{0,1:T(8,128)} async-done(((f32[128,128]{0,1:T(8,128)}), f32[128,2048]{0,1:T(8,128)}) %all-gather.7.cloned.1.call-update) | async-done | bytes 1048592 | tf_op jit(solution)/shard_map/all_gather | solution.py:44
  333.9 33.6 %all-gather.13.cloned.1.call-done = f32[2048,128]{1,0:T(8,128)} async-done(((f32[256,128]{1,0:T(8,128)}), f32[2048,128]{1,0:T(8,128)}) %all-gather.13.cloned.1.call-update) | async-done | bytes 1048592 | tf_op jit(solution)/shard_map/all_gather | solution.py:15
  367.5 4.0 fusion
  371.5 0.0 all-gather.15.cloned.1.call-update
  371.5 0.7 copy.11
  372.2 53.0 %all-gather.15.cloned.1.call-done = f32[128,2048]{0,1:T(8,128)} async-done(((f32[128,128]{0,1:T(8,128)}), f32[128,2048]{0,1:T(8,128)}) %all-gather.15.cloned.1.call-update) | async-done | bytes 1048592 | tf_op jit(solution)/shard_map/all_gather | solution.py:44
  425.2 0.0 copy-done
  425.2 3.7 fusion.4
  (2 shorter events, 0.1 us)
Async XLA Ops:
  7.2 0.7 copy-start.3
  7.2 93.8 %all-reduce.3.cloned.1.call-start = ((), (), s32[]{:S(2)}) async-start(), calls=%async_computation | async-start | bytes 524288 | tf_op jit(solution)/shard_map/psum | solution.py:27
  35.6 106.1 %all-reduce.5.cloned.1.call-start = ((), (), s32[]{:S(2)}) async-start(), calls=%async_computation.1 | async-start | bytes 524288 | tf_op jit(solution)/shard_map/psum | solution.py:27
  101.0 0.8 copy-start.2
  101.0 124.2 %all-gather.11.cloned.1.call-start = ((), (), s32[]{:S(2)}) async-start(), calls=%async_computation.4 | async-start | bytes 1179648 | tf_op jit(solution)/shard_map/all_gather | solution.py:15
  190.8 3.9 copy-start.1
  194.7 87.3 %all-gather.9.cloned.1.call-start = ((), (), s32[]{:S(2)}) async-start(), calls=%async_computation.3 | async-start | bytes 1114112 | tf_op jit(solution)/shard_map/all_gather | solution.py:44
  195.2 138.6 %all-gather.7.cloned.1.call-start = ((), (), s32[]{:S(2)}) async-start(), calls=%async_computation.2 | async-start | bytes 1114112 | tf_op jit(solution)/shard_map/all_gather | solution.py:44
  195.8 171.6 %all-gather.13.cloned.1.call-start = ((), (), s32[]{:S(2)}) async-start(), calls=%async_computation.5 | async-start | bytes 1179648 | tf_op jit(solution)/shard_map/all_gather | solution.py:15
  289.3 135.9 %copy-start = (f32[2048,128]{0,1:T(8,128)S(1)}, f32[2048,128]{0,1:T(8,128)}, u32[]{:S(2)}) copy-start(f32[2048,128]{0,1:T(8,128)} %all-gather.11.cloned.1.call-done) | copy-start | bytes 3145732
  289.3 135.9 %all-gather.15.cloned.1.call-start = ((), (), s32[]{:S(2)}) async-start(), calls=%async_computation.6 | async-start | bytes 1114112 | tf_op jit(solution)/shard_map/all_gather | solution.py:44
Sparse Core Ops, SparseCore 0:
  35.7 65.2 all-reduce.2
  103.5 38.0 all-reduce.4
  194.8 30.4 all-gather.10
  228.4 53.5 all-gather.8
  285.2 48.6 all-gather.6
  335.5 31.8 all-gather.12
  371.6 53.5 all-gather.14
